TPU v7x, 32 devices: a whole 2x2x4 slice. The times are simulated.
32 devices in a mesh: ep: 2 (over core), fsdp: 16 (over z, y, x).
Axes of the slice: x: 2, y: 2, z: 4, core: 2. Of those that a mesh axis runs over, the one named last changes fastest.
Arguments:
- train_down: float32 [8, 14336, 4096], P('ep', None, 'fsdp'), may hold values from -0.0625 to 0.0625
- router_weight: float32 [4096, 8], P('fsdp', 'ep'), may hold values from -0.09375 to 0.09375
- router_gain: float32 [4096], P('fsdp'), may hold values from 0.25 to 1.75
Outputs:
- ready_down: bfloat16 [8, 14336, 4096], P('ep', 'fsdp')
- scale_down: float32 [8, 14336], P('ep', 'fsdp')
- serve_router: bfloat16 [4096, 8], replicated
All inputs are finite; a program needn't handle non-finite values.
Results may differ from a plain program's by a relative error of at most 0.001.
Values may be sent and summed in bfloat16 or wider, within the bound.
A program may use at most 192 MiB of HBM per device.

v0:
```python
import jax
import jax.numpy as jnp
from jax import lax
from jax.sharding import PartitionSpec as P


def body(train_down, router_weight, router_gain):
    total_down = lax.psum(jnp.sum(train_down * train_down, axis=2), "fsdp")
    scale_down = jnp.sqrt(total_down)
    narrow_down = (train_down / jnp.expand_dims(scale_down, 2)).astype(jnp.bfloat16)
    ready_down = lax.all_to_all(narrow_down, "fsdp", split_axis=1, concat_axis=2, tiled=True)
    scale_down = lax.dynamic_slice_in_dim(
        scale_down, lax.axis_index("fsdp") * ready_down.shape[1], ready_down.shape[1], axis=1
    )
    part_router = (router_weight * router_gain[:, None]).astype(jnp.bfloat16)
    row_router = lax.all_gather(part_router, "fsdp", axis=0, tiled=True)
    serve_router = lax.all_gather(row_router, "ep", axis=1, tiled=True)
    return (ready_down, scale_down, serve_router)


def solution(mesh):
    placed = (P("ep", None, "fsdp"), P("fsdp", "ep"), P("fsdp"))
    return jax.shard_map(
        body,
        mesh=mesh,
        in_specs=placed,
        out_specs=(P("ep", "fsdp", None), P("ep", "fsdp"), P()),
        check_vma=False,
    )
```

profile of v0, /device:TPU:11, one launch (start us, length us, event | category | flops | bytes accessed | tf_op | source)
XLA Modules:
  0.0 972.7 jit_solution(4918430820290216060)
XLA Ops:
  7.2 0.0 all-reduce.2.cloned.1.call-start
  7.2 19.4 %multiply_reduce_fusion = f32[4,14336]{1,0:T(4,128)} fusion(f32[4,14336,256]{2,1,0:T(8,128)} %param.3), kind=kLoop, calls=%fused_computation.1 | loop fusion | flops 29302784 | bytes 58949632 | tf_op jit(solution)/shard_map/reduce_sum | solution.py:8
  26.6 0.0 all-reduce.2.cloned.1.call-update
  26.7 106.3 %all-reduce.2.cloned.1.call-done = f32[4,14336]{1,0:T(4,128)} async-done(((f32[4,14336]{1,0:T(4,128)}), f32[4,14336]{1,0:T(4,128)}) %all-reduce.2.cloned.1.call-update) | async-done | bytes 229392 | tf_op jit(solution)/shard_map/psum | solution.py:8
  132.9 1.0 sqrt.3
  134.0 4.7 copy.7
  138.6 0.0 copy-start
  138.6 0.0 copy-start.1
  138.6 65.1 %fusion = bf16[4,14336,256]{2,0,1:T(4,128)(2,1)} fusion(f32[4,14336,256]{2,1,0:T(8,128)} %param.3, f32[4,14336]{0,1:T(8,128)} %copy.7), kind=kLoop, calls=%fused_computation.2 | loop fusion | flops 29360128 | bytes 88309760 | tf_op jit(solution)/shard_map/convert_element_type | solution.py:10
  203.8 6.1 all-to-all-start
  209.9 0.0 copy-done
  209.9 0.0 copy-done.1
  209.9 672.0 %all_gather.6 = bf16[4096,4]{0,1:T(4,128)(2,1)S(1)} all-gather(bf16[256,4]{0,1:T(4,128)(2,1)S(1)} %multiply_convert_fusion), channel_id=1, replica_groups=mesh['ep'=2,'fsdp'=16] {'fsdp'}, dimensions={0}, use_global_device_ids=true | all-gather | bytes 34816 | tf_op jit(solution)/shard_map/all_gather | solution.py:16
  881.9 11.4 %all-gather = bf16[2,4,4096]{2,1,0:T(4,128)(2,1)S(1)} all-gather(bf16[1,4,4096]{2,1,0:T(4,128)(2,1)S(1)} %bitcast.9), channel_id=1, replica_groups=mesh['ep'=2,'fsdp'=16] {'ep'}, dimensions={0}, use_global_device_ids=true | all-gather | bytes 98304 | tf_op jit(solution)/shard_map/all_gather | solution.py:17
  893.3 0.7 reshape.9
  894.0 0.6 constant_dynamic-slice_fusion
  894.6 0.0 all-to-all-done
  894.6 27.5 %copy.9 = bf16[4,896,16,256]{3,2,1,0:T(8,128)(2,1)} copy(bf16[4,896,16,256]{3,0,1,2:T(4,128)(2,1)} %bitcast.1) | data formatting | bytes 58720256 | tf_op jit(solution)/shard_map/all_to_all | solution.py:11
  922.1 43.7 %all_to_all.16 = bf16[4,896,4096]{2,1,0:T(8,128)(2,1)} reshape(bf16[4,896,16,256]{3,2,1,0:T(8,128)(2,1)} %copy.9) | data formatting | bytes 58720256 | tf_op jit(solution)/shard_map/all_to_all | solution.py:11
  (1 shorter events, 0.0 us)
Async XLA Ops:
  7.2 125.8 %all-reduce.2.cloned.1.call-start = ((), (), s32[]{:S(2)}) async-start(), calls=%async_computation.1 | async-start | bytes 458752 | tf_op jit(solution)/shard_map/psum | solution.py:8
  138.6 71.3 %copy-start = (f32[256,4]{0,1:T(4,128)S(1)}, f32[256,4]{0,1:T(4,128)}, u32[]{:S(2)}) copy-start(f32[256,4]{0,1:T(4,128)} %param.4) | copy-start | bytes 12292
  138.6 71.3 %copy-start.1 = (f32[256]{0:T(256)S(1)}, f32[256]{0:T(256)}, u32[]{:S(2)}) copy-start(f32[256]{0:T(256)} %param.5) | copy-start | bytes 3076
  203.8 690.8 %all-to-all-start = ((bf16[4,14336,256]{2,0,1:T(4,128)(2,1)}), bf16[4,14336,256]{2,0,1:T(4,128)(2,1)}, u32[]{:S(2)}, u32[]{:S(2)}) async-start(bf16[4,14336,256]{2,0,1:T(4,128)(2,1)} %fusion), calls=%async_computation | async-start | bytes 58720256 | tf_op jit(solution)/shard_map/all_to_all | solution.py:11
Sparse Core Ops, SparseCore 0:
  26.8 106.1 all-reduce.1
where the time goes:
time: 974 us; the launch traced here: 973 us
  blocking collectives  683 us (70%)
  waiting for transfers between devices  106 us (11%)
  other arithmetic  84.6 us (9%)
  local copies, waits for them, and re-layouts  78.2 us (8%)
  between operations  14.1 us (1%)
    all_gather x1, blocking collectives, body(): row_router = lax.all_gather(part_router, 'fsdp', axis=0, tiled=True)  672 us
    psum x1, waiting for transfers between devices, body(): total_down = lax.psum(jnp.sum(train_down * train_down, axis=2), 'fsdp')  106 us
    all_to_all x2, local copies, waits for them, and re-layouts, body(): lax.all_to_all(narrow_down, 'fsdp', split_axis=1, concat_axis=2, tiled=True)  71.2 us
    convert_element_type x1, other arithmetic, body(): (train_down / jnp.expand_dims(scale_down, 2)).astype(jnp.bfloat16)  65.1 us
  transfers between devices with their start and end apart: 2, of which 1 were waited for; matrix products, arithmetic and copies ran while one was open for 0% of the time, Pallas kernels for 0%

commit v1 on v0

v1 whole, which is shorter than its diff:
```python
import functools

import jax
import jax.numpy as jnp
from jax import lax
from jax.experimental import pallas as pl
from jax.experimental.pallas import tpu as pltpu
from jax.sharding import PartitionSpec as P

MESH = pl.DeviceIdType.MESH
BUFFERS = 4


def kernel(n, g, w_ref, part_ref, ready_ref, scale_ref, router_ref, wbuf, stage, sums, wide, sent, got, inv, gathered,
           wsem, send, recv, rs_send, rs_recv, ag_send, ag_recv, ro_send, ro_recv, ro_own):
    experts, _, width = w_ref.shape
    rows = stage.shape[1]
    blocks = experts * n
    chunk = 64 if rows % 64 == 0 else 8
    lanes = sums.shape[1]
    me, group = lax.axis_index("fsdp"), lax.axis_index("ep")
    flat = group * n + me
    everyone = g * n

    def device(index):
        return {"ep": index // n, "fsdp": index % n}

    def partner(k):
        if n & (n - 1):
            return (me + k) % n
        found, bit = 0, 1
        while bit < n:
            found = found + (((me // bit) % 2 + (k // bit) % 2) % 2) * bit
            bit *= 2
        return found

    def distance(t):
        j = t % n
        return n - 1 - j // 2 - (j % 2) * (n // 2)

    def load(expert, owner, slot):
        return pltpu.make_async_copy(w_ref.at[expert, pl.ds(owner * rows, rows), :], wbuf.at[slot], wsem.at[slot])

    def load_sum(t):
        return load(t % experts, t // experts, t % BUFFERS)

    def load_scale(t):
        return load(t // n, partner(distance(t)), t % BUFFERS)

    for t in range(min(BUFFERS - 1, blocks)):
        load_sum(t).start()

    barrier = pltpu.get_barrier_semaphore()

    @pl.loop(1, everyone)
    def _(q):
        pl.semaphore_signal(barrier, inc=1, device_id=device((flat + q) % everyone), device_id_type=MESH)

    pl.semaphore_wait(barrier, everyone - 1)

    def router_copy(q):
        return pltpu.make_async_remote_copy(
            src_ref=part_ref, dst_ref=router_ref.at[group, me], send_sem=ro_send.at[q], recv_sem=ro_recv.at[q],
            device_id=device((flat + q) % everyone), device_id_type=MESH)

    own_router = pltpu.make_async_copy(part_ref, router_ref.at[group, me], ro_own)
    own_router.start()

    sums[...] = jnp.zeros_like(sums)

    @pl.loop(0, blocks)
    def _(t):
        @pl.when(t + BUFFERS - 1 < blocks)
        def _():
            load_sum(t + BUFFERS - 1).start()

        load_sum(t).wait()
        slot = t % BUFFERS

        @pl.loop(0, rows // chunk)
        def _(c):
            at = pl.ds(pl.multiple_of(c * chunk, chunk), chunk)
            x = wbuf[slot, at, :]
            total = jnp.sum(x * x, axis=1, keepdims=True)
            lane = lax.broadcasted_iota(jnp.int32, (chunk, lanes), 1)
            sums[at, :] = jnp.where(lane == t, total, sums[at, :])

    for t in range(min(BUFFERS - 1, blocks)):
        load_scale(t).start()

    wide[...] = sums[...].T
    for d in range(n):
        sent[d] = wide[d * experts:(d + 1) * experts, :]

    def scatter_copy(k):
        other = partner(k)
        return pltpu.make_async_remote_copy(
            src_ref=sent.at[other], dst_ref=got.at[k], send_sem=rs_send.at[k], recv_sem=rs_recv.at[k],
            device_id={"fsdp": other}, device_id_type=MESH)

    def gather_copy(k):
        return pltpu.make_async_remote_copy(
            src_ref=inv, dst_ref=gathered.at[me], send_sem=ag_send.at[k], recv_sem=ag_recv.at[k],
            device_id={"fsdp": partner(k)}, device_id_type=MESH)

    @pl.loop(1, n)
    def _(k):
        scatter_copy(n - k).start()

    total = sent[me]
    got[0] = total
    for k in range(1, n):
        scatter_copy(k).wait_recv()
        total = total + got[k]
    scale = jnp.sqrt(total)
    scale_ref[...] = scale
    inv[...] = 1.0 / scale
    gathered[me] = inv[...]

    @pl.loop(1, n)
    def _(k):
        gather_copy(n - k).start()

    @pl.loop(1, n)
    def _(k):
        gather_copy(k).wait_recv()

    for d in range(n):
        wide[d * experts:(d + 1) * experts, :] = gathered[d]
    sums[...] = wide[...].T

    def piece(t):
        return ready_ref.at[t // n, :, pl.ds(pl.multiple_of(me * width, width), width)]

    def send_copy(t):
        return pltpu.make_async_remote_copy(
            src_ref=stage.at[t], dst_ref=piece(t), send_sem=send.at[t], recv_sem=recv.at[t],
            device_id={"fsdp": partner(distance(t))}, device_id_type=MESH)

    def keep_copy(t):
        return pltpu.make_async_copy(stage.at[t], piece(t), send.at[t])

    def issue(t):
        @pl.when(t % n != n - 1)
        def _():
            send_copy(t).start()

        @pl.when(t % n == n - 1)
        def _():
            keep_copy(t).start()

    @pl.loop(0, blocks)
    def _(t):
        @pl.when(t + BUFFERS - 1 < blocks)
        def _():
            load_scale(t + BUFFERS - 1).start()

        load_scale(t).wait()
        slot = t % BUFFERS
        column = partner(distance(t)) * experts + t // n

        @pl.loop(0, rows // chunk)
        def _(c):
            at = pl.ds(pl.multiple_of(c * chunk, chunk), chunk)
            lane = lax.broadcasted_iota(jnp.int32, (chunk, lanes), 1)
            factor = jnp.sum(jnp.where(lane == column, sums[at, :], 0.0), axis=1, keepdims=True)
            stage[t, at, :] = (wbuf[slot, at, :] * factor).astype(jnp.bfloat16)

        @pl.when(t > 0)
        def _():
            issue(t - 1)

    issue(blocks - 1)

    @pl.loop(1, everyone)
    def _(q):
        router_copy(q).start()

    @pl.loop(1, n)
    def _(k):
        scatter_copy(k).wait_send()
        gather_copy(k).wait_send()

    @pl.loop(0, blocks)
    def _(t):
        @pl.when(t % n != n - 1)
        def _():
            send_copy(t).wait_send()
            send_copy(t).wait_recv()

        @pl.when(t % n == n - 1)
        def _():
            keep_copy(t).wait()

    @pl.loop(1, everyone)
    def _(q):
        router_copy(q).wait_send()
        router_copy(q).wait_recv()

    own_router.wait()


def body(n, g, train_down, router_weight, router_gain):
    experts, length, width = train_down.shape
    rows, blocks = length // n, experts * n
    lanes = -(-blocks // 128) * 128
    part = (router_weight * router_gain[:, None]).astype(jnp.bfloat16).astype(jnp.float32).T
    dma = pltpu.SemaphoreType.DMA
    vmem = pl.BlockSpec(memory_space=pltpu.VMEM)
    hbm = pl.BlockSpec(memory_space=pl.ANY)
    ready, scale, router = pl.pallas_call(
        functools.partial(kernel, n, g),
        out_shape=(
            jax.ShapeDtypeStruct((experts, rows, n * width), jnp.bfloat16),
            jax.ShapeDtypeStruct((experts, rows), jnp.float32),
            jax.ShapeDtypeStruct((g, n) + part.shape, jnp.float32),
        ),
        in_specs=[hbm, vmem],
        out_specs=(hbm, vmem, hbm),
        scratch_shapes=[
            pltpu.VMEM((BUFFERS, rows, width), jnp.float32),
            pltpu.VMEM((blocks, rows, width), jnp.bfloat16),
            pltpu.VMEM((rows, lanes), jnp.float32),
            pltpu.VMEM((lanes, rows), jnp.float32),
            pltpu.VMEM((n, experts, rows), jnp.float32),
            pltpu.VMEM((n, experts, rows), jnp.float32),
            pltpu.VMEM((experts, rows), jnp.float32),
            pltpu.VMEM((n, experts, rows), jnp.float32),
            dma((BUFFERS,)),
            dma((blocks,)),
            dma((blocks,)),
            dma((n,)),
            dma((n,)),
            dma((n,)),
            dma((n,)),
            dma((n * g,)),
            dma((n * g,)),
            dma,
        ],
        compiler_params=pltpu.CompilerParams(collective_id=0, has_side_effects=True, vmem_limit_bytes=60 * 2**20),
    )(train_down, part)
    router = router.transpose(1, 3, 0, 2).reshape(n * part.shape[1], g * experts)
    return ready, scale, router.astype(jnp.bfloat16)


def solution(mesh):
    placed = (P("ep", None, "fsdp"), P("fsdp", "ep"), P("fsdp"))
    return jax.shard_map(
        functools.partial(body, mesh.shape["fsdp"], mesh.shape["ep"]),
        mesh=mesh,
        in_specs=placed,
        out_specs=(P("ep", "fsdp", None), P("ep", "fsdp"), P()),
        check_vma=False,
    )
```

time: 974 us -> 792 us (0.81)
  Pallas kernels: 0 us -> 765 us
  blocking collectives: 683 us -> 0 us
  waiting for transfers between devices: 106 us -> 0 us
  other arithmetic: 84.6 us -> 2.22 us
  local copies, waits for them, and re-layouts: 78.2 us -> 21.3 us
  between operations: 14.1 us -> 0.65 us
    pallas_call x0 -> x1, Pallas kernels: none -> 765 us  [body(): pl.pallas_call(functools.partial(kernel, n, g), out_shape=(jax.ShapeDtype...]
    all_gather x2 -> x0, blocking collectives: 683 us -> none  [the longest x1 672 us: body(): row_router = lax.all_gather(part_router, 'fsdp', axis=0, tiled=True)]
    psum x1 -> x0, waiting for transfers between devices: 106 us -> none  [body(): total_down = lax.psum(jnp.sum(train_down * train_down, axis=2), 'fsdp')]
    all_to_all x2 -> x0, local copies, waits for them, and re-layouts: 71.2 us -> none  [body(): lax.all_to_all(narrow_down, 'fsdp', split_axis=1, concat_axis=2, tiled=True)]
    convert_element_type x2 -> x1, other arithmetic: 65.1 us -> 0.93 us  [body(): return (ready, scale, router.astype(jnp.bfloat16))]
    unnamed x5, local copies, waits for them, and re-layouts: 0.66 us -> 21.3 us
    reduce_sum x1 -> x0, other arithmetic: 19.4 us -> none  [body(): total_down = lax.psum(jnp.sum(train_down * train_down, axis=2), 'fsdp')]
  transfers between devices with their start and end apart: 2 -> 0, of which waited for: 1 -> 0; matrix products, arithmetic and copies ran while one was open for 0% -> 0% of each run, Pallas kernels for 0% -> 0%
where the time goes in v1:
time: 792 us; the launch traced here: 789 us
  Pallas kernels  765 us (97%)
  local copies, waits for them, and re-layouts  21.3 us (3%)
    pallas_call x1, Pallas kernels, body(): pl.pallas_call(functools.partial(kernel, n, g), out_shape=(jax.ShapeDtype...  765 us
    unnamed x5, local copies, waits for them, and re-layouts  21.3 us

profile of v1, /device:TPU:11, one launch (start us, length us, event | category | flops | bytes accessed | tf_op | source)
XLA Modules:
  0.0 788.9 jit_solution(12844872675328059480)
XLA Ops:
  0.6 1.3 convert_bitcast_fusion.1.part_ref
  1.9 764.7 %shard_map.58 = (bf16[4,896,4096]{2,1,0:T(8,128)(2,1)}, f32[4,896]{1,0:T(4,128)}, f32[2,16,4,256]{3,2,1,0:T(4,128)}) custom-call(f32[4,14336,256]{2,1,0:T(8,128)} %w_ref.1, f32[4,256]{1,0:T(4,128)} %convert_bitcast_fusion.1.part_ref), custom_call_target="tpu_custom_call" | custom-call | tf_op jit(solution)/shard_map/pallas_call | solution.py:211
  766.6 0.9 convert_bitcast_fusion
  767.6 0.7 copy.7
  768.2 0.0 copy-start
  768.2 20.0 %copy.10 = bf16[4,896,4096]{2,1,0:T(8,128)(2,1)} copy(bf16[4,896,4096]{2,1,0:T(8,128)(2,1)} %get-tuple-element.12) | data formatting | bytes 58720256
  788.3 0.0 copy-done
  788.3 0.6 copy.11
  (1 shorter events, 0.0 us)
Async XLA Ops:
  768.2 20.0 %copy-start = (f32[4,896]{1,0:T(4,128)S(1)}, f32[4,896]{1,0:T(4,128)}, u32[]{:S(2)}) copy-start(f32[4,896]{1,0:T(4,128)} %get-tuple-element.13) | copy-start | bytes 43012

commit v2 on v1

--- a/solution.py
+++ b/solution.py
@@ -130,7 +130,7 @@
     sums[...] = wide[...].T
 
     def piece(t):
-        return ready_ref.at[t // n, :, pl.ds(pl.multiple_of(me * width, width), width)]
+        return ready_ref.at[t // n, me]
 
     def send_copy(t):
         return pltpu.make_async_remote_copy(
@@ -198,6 +198,24 @@
         router_copy(q).wait_recv()
 
     own_router.wait()
+
+
+def join_kernel(pieces_ref, joined_ref):
+    n, width = pieces_ref.shape[1], pieces_ref.shape[3]
+    for d in range(n):
+        joined_ref[0, :, d * width:(d + 1) * width] = pieces_ref[0, d]
+
+
+def join(pieces):
+    experts, n, rows, width = pieces.shape
+    tile = next(size for size in (128, 64, rows) if rows % size == 0)
+    return pl.pallas_call(
+        join_kernel,
+        grid=(experts, rows // tile),
+        in_specs=[pl.BlockSpec((1, n, tile, width), lambda e, r: (e, 0, r, 0))],
+        out_specs=pl.BlockSpec((1, tile, n * width), lambda e, r: (e, r, 0)),
+        out_shape=jax.ShapeDtypeStruct((experts, rows, n * width), pieces.dtype),
+    )(pieces)
 
 
 def body(n, g, train_down, router_weight, router_gain):
@@ -211,7 +229,7 @@
     ready, scale, router = pl.pallas_call(
         functools.partial(kernel, n, g),
         out_shape=(
-            jax.ShapeDtypeStruct((experts, rows, n * width), jnp.bfloat16),
+            jax.ShapeDtypeStruct((experts, n, rows, width), jnp.bfloat16),
             jax.ShapeDtypeStruct((experts, rows), jnp.float32),
             jax.ShapeDtypeStruct((g, n) + part.shape, jnp.float32),
         ),
@@ -240,7 +258,7 @@
         compiler_params=pltpu.CompilerParams(collective_id=0, has_side_effects=True, vmem_limit_bytes=60 * 2**20),
     )(train_down, part)
     router = router.transpose(1, 3, 0, 2).reshape(n * part.shape[1], g * experts)
-    return ready, scale, router.astype(jnp.bfloat16)
+    return join(ready), scale, router.astype(jnp.bfloat16)
 
 
 def solution(mesh):

time: 792 us -> 803 us (1.014)
  Pallas kernels: 765 us -> 795 us
  local copies, waits for them, and re-layouts: 21.3 us -> 1.27 us
    pallas_call x0 -> x1, Pallas kernels: none -> 30.6 us  [join(): pl.pallas_call(join_kernel, grid=(experts, rows // tile), in_specs=[pl.Bl...]
    unnamed x5 -> x6, local copies, waits for them, and re-layouts: 21.3 us -> 1.26 us
where the time goes in v2:
time: 803 us; the launch traced here: 799 us
  Pallas kernels  795 us (99%)
    pallas_call x1, Pallas kernels, body(): pl.pallas_call(functools.partial(kernel, n, g), out_shape=(jax.ShapeDtype...  765 us
    pallas_call x1, Pallas kernels, join(): pl.pallas_call(join_kernel, grid=(experts, rows // tile), in_specs=[pl.Bl...  30.6 us

profile of v2, /device:TPU:11, one launch (start us, length us, event | category | flops | bytes accessed | tf_op | source)
XLA Modules:
  0.0 798.6 jit_solution(16530682364577999099)
XLA Ops:
  0.6 1.3 convert_bitcast_fusion.1.part_ref
  1.9 764.7 %shard_map.58 = (bf16[4,16,896,256]{3,2,1,0:T(8,128)(2,1)}, f32[4,896]{1,0:T(4,128)}, f32[2,16,4,256]{3,2,1,0:T(4,128)}) custom-call(f32[4,14336,256]{2,1,0:T(8,128)} %w_ref.1, f32[4,256]{1,0:T(4,128)} %convert_bitcast_fusion.1.part_ref), custom_call_target="tpu_custom_call" | custom-call | tf_op jit(solution)/shard_map/pallas_call | solution.py:229
  766.6 0.0 copy-start
  766.6 0.0 copy-start.1
  766.6 30.6 %shard_map.59 = bf16[4,896,4096]{2,1,0:T(8,128)(2,1)} custom-call(bf16[4,16,896,256]{3,2,1,0:T(8,128)(2,1)} %get-tuple-element.6.pieces_ref), custom_call_target="tpu_custom_call" | custom-call | tf_op jit(solution)/shard_map/pallas_call | solution.py:212
  797.3 0.0 copy-done
  797.3 0.7 copy.7
  798.0 0.0 copy-done.1
  798.0 0.6 copy.9
  (2 shorter events, 0.0 us)
Async XLA Ops:
  766.6 30.7 %copy-start = (f32[2,16,4,256]{3,2,1,0:T(4,128)S(1)}, f32[2,16,4,256]{3,2,1,0:T(4,128)}, u32[]{:S(2)}) copy-start(f32[2,16,4,256]{3,2,1,0:T(4,128)} %get-tuple-element.8) | copy-start | bytes 393220
  766.6 31.4 %copy-start.1 = (f32[4,896]{1,0:T(4,128)S(1)}, f32[4,896]{1,0:T(4,128)}, u32[]{:S(2)}) copy-start(f32[4,896]{1,0:T(4,128)} %get-tuple-element.13) | copy-start | bytes 43012
